TPU v7x, 32 devices: a whole 2x2x4 slice. The times are simulated.
32 devices in a mesh: gx: 4 (over y, core), gy: 8 (over z, x).
Axes of the slice: x: 2, y: 2, z: 4, core: 2. Of those that a mesh axis runs over, the one named last changes fastest.
Arguments:
- populations: float32 [19, 16, 64, 128], P(None, 'gx', 'gy'), may hold values from 0.004 to 0.8, as said below
- solid: int32 [16, 64, 128], P('gx', 'gy'), may hold values 0 or 1
- base_cell: int32 [3, 4, 8, 2, 768], P(None, 'gx', 'gy'), may hold values from 0 to 127, as said below
- offset: float32 [3, 4, 8, 2, 768], P(None, 'gx', 'gy'), may hold values from 0 to 1
- rest_displacement: float32 [3, 4, 8, 2, 768], P(None, 'gx', 'gy'), may hold values from 0 to 1
- stiffness: float32 [4, 8, 2], P('gx', 'gy'), may hold values from 0.006380062 to 0.063800626
- occupied: int32 [4, 8, 2], P('gx', 'gy'), may hold values from 0 to 1, as said below
- triangles: int32 [1280, 3], replicated, may hold values from 0 to 641, as said below
Outputs:
- populations_out: float32 [19, 16, 64, 128], P(None, 'gx', 'gy')
- offset_out: float32 [3, 4, 8, 2, 768], P(None, 'gx', 'gy')
Inputs may be any that keep to these rules, and one draw needn't show every extreme that they name: `populations`: every entry is positive. `base_cell`: component 0 of a vertex stored at index i of gx lies in [i * 4, (i + 1) * 4), component 1 of one stored at index j of gy lies in [j * 8, (j + 1) * 8), component 2 lies below 128. The occupied slots of a device come first; each device has at least one, and some device has all 2. `triangles`: each row holds three different vertex numbers below 642.
All inputs are finite; a program needn't handle non-finite values. No bound on the sum of `solid` on one device may be relied on, other than what follows from the above.
Results may differ from a plain program's by a relative error of at most 0.0001.
Values sent between devices are 32-bit elements; how exact they have to be, the bound alone decides.
A program may use at most 64 MiB of HBM per device.

v0:
```python
import functools
import math

import jax
import jax.numpy as jnp
from jax import lax
from jax.experimental import pallas as pl
from jax.experimental.pallas import tpu as pltpu
from jax.sharding import PartitionSpec as P

SUBSTEPS = 3
VELOCITIES = [
    (0, 0, 0), (1, 0, 0), (-1, 0, 0), (0, 1, 0), (0, -1, 0), (0, 0, 1), (0, 0, -1),
    (1, 1, 0), (-1, -1, 0), (1, -1, 0), (-1, 1, 0), (1, 0, 1), (-1, 0, -1), (1, 0, -1),
    (-1, 0, 1), (0, 1, 1), (0, -1, -1), (0, 1, -1), (0, -1, 1),
]
OPPOSITE = [0, 2, 1, 4, 3, 6, 5, 8, 7, 10, 9, 12, 11, 14, 13, 16, 15, 18, 17]
LATTICE_WEIGHTS = [1.0 / 3.0] + [1.0 / 18.0] * 6 + [1.0 / 36.0] * 12
RELAX = 0.8
XS = {s: [q for q in range(19) if VELOCITIES[q][0] == s] for s in (1, -1)}
YS = {s: [q for q in range(19) if VELOCITIES[q][1] == s] for s in (1, -1)}
CORNER = {(v[0], v[1]): q for q, v in enumerate(VELOCITIES) if v[0] and v[1]}
DIRS = [(1, 0), (-1, 0), (0, 1), (0, -1), (1, 1), (1, -1), (-1, 1), (-1, -1)]
MESH = pl.DeviceIdType.MESH
NT = (((1,), (1,)), ((), ()))
NN = (((1,), (0,)), ((), ()))


def mm(a, b, dims):
    return lax.dot_general(a, b, dims, preferred_element_type=jnp.float32)


def split(value):
    high = value.astype(jnp.bfloat16)
    low = (value - high.astype(jnp.float32)).astype(jnp.bfloat16)
    return high, low


def quarter_sine(t):
    t = t - 4.0 * jnp.floor(t * 0.25 + 0.5)
    t = jnp.where(t > 1.0, 2.0 - t, jnp.where(t < -1.0, -2.0 - t, t))
    x = t * (math.pi / 2.0)
    u = x * x
    p = 1.0 / 6227020800.0
    for c in (-1.0 / 39916800.0, 1.0 / 362880.0, -1.0 / 5040.0, 1.0 / 120.0, -1.0 / 6.0, 1.0):
        p = p * u + c
    return x * p


def table(rows, base, kernels):
    cells = lax.broadcasted_iota(jnp.int32, (rows, base.shape[1]), 0)
    d = (cells - base + 1) & (rows - 1)
    out = jnp.where(d == 3, kernels[3], 0.0)
    for s in (2, 1, 0):
        out = jnp.where(d == s, kernels[s], out)
    return out


def moments(pops):
    density = functools.reduce(lambda a, b: a + b, pops)
    momentum = []
    for a in range(3):
        plus = [pops[q] for q in range(19) if VELOCITIES[q][a] == 1]
        minus = [pops[q] for q in range(19) if VELOCITIES[q][a] == -1]
        momentum.append(
            functools.reduce(lambda a, b: a + b, plus)
            - functools.reduce(lambda a, b: a + b, minus)
        )
    return density, momentum


def collide(pops, force, walled):
    density, momentum = moments(pops)
    inverse = 1.0 / density
    u = [(momentum[a] + 0.5 * force[a]) * inverse for a in range(3)]
    squared = u[0] * u[0] + u[1] * u[1] + u[2] * u[2]
    working = u[0] * force[0] + u[1] * force[1] + u[2] * force[2]
    base = 1.0 - 1.5 * squared
    relaxed = []
    for q in range(19):
        vector = VELOCITIES[q]
        along, pushed = jnp.zeros_like(density), jnp.zeros_like(density)
        for a in range(3):
            if vector[a] == 1:
                along, pushed = along + u[a], pushed + force[a]
            elif vector[a] == -1:
                along, pushed = along - u[a], pushed - force[a]
        w = LATTICE_WEIGHTS[q]
        equilibrium = (w * density) * (base + along * (3.0 + 4.5 * along))
        source = ((1.0 - 0.5 / RELAX) * w) * (3.0 * (pushed - working) + 9.0 * along * pushed)
        updated = pops[q] - (pops[q] - equilibrium) * (1.0 / RELAX) + source
        relaxed.append(jnp.where(walled, pops[OPPOSITE[q]], updated))
    return relaxed


def roll(x, shift, axis):
    size = x.shape[axis]
    shift = shift % size
    return x if shift == 0 else pltpu.roll(x, shift, axis)


def body_kernel(
    peers_x, peers_y,
    pops_ref, solid_ref, base_ref, offset_ref, rest_ref, stiff_ref, occ_ref, tri_ref,
    pops_out, offset_out,
    inc, lap, off, spread, grid, out_pops, out_flow, wide,
    *scratch,
):
    recv_force, recv_pops, recv_flow = scratch[0:8], scratch[8:16], scratch[16:24]
    send_px, send_py, send_pc = scratch[24:26], scratch[26:28], scratch[28:32]
    send_sem, recv_sem = scratch[32:34]
    rows_x = pops_ref.shape[1]
    depth = pops_ref.shape[3]
    slots, padded = base_ref.shape[1], base_ref.shape[2]
    vertices = slots * padded
    planes = rows_x + 3
    ix, iy = lax.axis_index("gx"), lax.axis_index("gy")
    peer = [((ix + sx + peers_x) % peers_x, (iy + sy + peers_y) % peers_y) for sx, sy in DIRS]

    barrier = pltpu.get_barrier_semaphore()
    for p in peer:
        pl.semaphore_signal(barrier, inc=1, device_id=p, device_id_type=MESH)

    ids = lax.broadcasted_iota(jnp.int32, inc.shape, 0)
    hit = (ids == tri_ref[0:1, :]) | (ids == tri_ref[1:2, :]) | (ids == tri_ref[2:3, :])
    inc[...] = jnp.where(hit, 1.0, 0.0).astype(jnp.bfloat16)
    pairs = mm(inc[...], inc[...], NT)
    same = lax.broadcasted_iota(jnp.int32, pairs.shape, 0) == lax.broadcasted_iota(
        jnp.int32, pairs.shape, 1
    )
    lap_high, lap_low = split(jnp.where(same, -2.0 * pairs, pairs))
    lap[0] = lap_high
    lap[1] = lap_low

    def flat(ref):
        return jnp.concatenate([ref[:, m, :] for m in range(slots)], axis=1)

    base = flat(base_ref)
    base_x = base[0:1] - ix * rows_x
    base_y = base[1:2] - iy * pops_ref.shape[2]
    base_z = base[2:3]
    live = jnp.concatenate(
        [jnp.full((1, padded), occ_ref[m].astype(jnp.float32)) for m in range(slots)], axis=1
    )
    scale = live * jnp.concatenate(
        [jnp.full((1, padded), stiff_ref[m]) for m in range(slots)], axis=1
    )
    off[...] = flat(offset_ref)
    pops_out[...] = pops_ref[...]
    sub = lax.broadcasted_iota(jnp.int32, (8, depth), 0)
    pl.semaphore_wait(barrier, len(peer))

    def copy(step, stage, d, src, dst):
        return pltpu.make_async_remote_copy(
            src_ref=src, dst_ref=dst.at[step], send_sem=send_sem.at[step, stage, d],
            recv_sem=recv_sem.at[step, stage, d], device_id=peer[d], device_id_type=MESH,
        )

    def force_copies(step):
        part = {1: pl.ds(rows_x, 2), -1: pl.ds(rows_x + 2, 1), 0: pl.ds(0, rows_x)}
        return [
            copy(step, 0, d, grid.at[step, part[sx], :, 0 if sy == 0 else 1], recv_force[d])
            for d, (sx, sy) in enumerate(DIRS)
        ]

    def pops_copies(step):
        src = list(send_px) + list(send_py) + list(send_pc)
        return [copy(step, 1, d, src[d].at[step], recv_pops[d]) for d in range(8)]

    def flow_copies(step):
        part = {1: pl.ds(rows_x - 1, 1), -1: pl.ds(0, 2), 0: pl.ds(0, rows_x)}
        return [
            copy(step, 2, d, out_flow.at[step, part[sx]], recv_flow[d])
            for d, (sx, sy) in enumerate(DIRS)
        ]

    def substep(step, carry):
        now = off[...]
        strain = now - flat(rest_ref)
        six = jnp.concatenate(
            [strain[:, m * padded : (m + 1) * padded] for m in range(slots)], axis=0
        )
        six_high = six.astype(jnp.bfloat16).astype(jnp.float32)
        both = jnp.concatenate([six_high, six - six_high], axis=0).astype(jnp.bfloat16)
        pulled = mm(both, lap[0], NN) + mm(both, lap[1], NN)
        pulled = pulled[0 : 3 * slots] + pulled[3 * slots :]
        force_v = scale * jnp.concatenate(
            [pulled[3 * m : 3 * m + 3] for m in range(slots)], axis=1
        )
        s = quarter_sine(now) * 0.25
        c = quarter_sine(now + 1.0) * 0.25
        kernels = (0.25 - s, 0.25 + c, 0.25 + s, 0.25 - c)
        table_x = table(8, base_x, [k[0:1] for k in kernels])
        table_y = table(16, base_y, [k[1:2] for k in kernels])
        deep_high, deep_low = split(table(depth, base_z, [k[2:3] for k in kernels]))
        deep = jnp.concatenate([deep_high, deep_low], axis=0)
        order = list(range(rows_x + 2)) + [7]
        for i, x in enumerate(order):
            for a in range(3):
                block = (force_v[a : a + 1] * table_x[x : x + 1]) * table_y
                high, low = split(block)
                row = (3 * i + a) * 16
                spread[0, row : row + 16, :] = high
                spread[1, row : row + 16, :] = low
        first = mm(spread[0], deep, NT)
        total = first[:, :depth] + first[:, depth:] + mm(spread[1], deep_high, NT)
        grid[step] = total.reshape(planes, 3, 2, 8, depth)
        sends = force_copies(step)
        for x in sends:
            x.start()
        for x in sends:
            x.wait_recv()
        R = {dv: recv_force[d][step] for d, dv in enumerate(DIRS)}
        low_rows = sub < 4
        total = grid[step, 0:rows_x, :, 0] + jnp.where(low_rows, R[0, 1], R[0, -1])
        left = R[1, 0] + jnp.where(low_rows, R[1, 1], R[1, -1])
        right = R[-1, 0] + jnp.where(low_rows, R[-1, 1], R[-1, -1])
        total = jnp.concatenate(
            [total[0:2] + left, total[2 : rows_x - 1], total[rows_x - 1 :] + right], axis=0
        )
        force = [total[:, a] for a in range(3)]

        relaxed = collide([pops_out[q] for q in range(19)], force, solid_ref[...] != 0)
        moved = [
            roll(roll(relaxed[q], VELOCITIES[q][2], 2), VELOCITIES[q][1], 1) for q in range(19)
        ]
        for n, sx in enumerate((1, -1)):
            edge = rows_x - 1 if sx == 1 else 0
            for k, q in enumerate(XS[sx]):
                send_px[n][step, k] = moved[q][edge]
        for n, sy in enumerate((1, -1)):
            packed = moved[YS[sy][0]]
            start = 0 if sy == 1 else 7
            for k, q in enumerate(YS[sy][1:], 1):
                packed = jnp.where(sub == (start + k) % 8, roll(moved[q], k, 1), packed)
            send_py[n][step] = packed
        for n, (sx, sy) in enumerate(DIRS[4:]):
            send_pc[n][step] = moved[CORNER[sx, sy]][rows_x - 1 if sx == 1 else 0]
        sends = pops_copies(step)
        for x in sends:
            x.start()
        for x in sends:
            x.wait_recv()
        from_y = {1: recv_pops[2][step], -1: recv_pops[3][step]}
        fresh = []
        for q in range(19):
            sx, sy, _ = VELOCITIES[q]
            value = moved[q]
            edge_row = sub == (0 if sy == 1 else 7)
            if sy:
                value = jnp.where(edge_row, roll(from_y[sy], -YS[sy].index(q), 1), value)
            if sx:
                side = recv_pops[0 if sx == 1 else 1][step, XS[sx].index(q)]
                if sy:
                    side = jnp.where(edge_row, recv_pops[DIRS.index((sx, sy))][step], side)
                if sx == 1:
                    value = jnp.concatenate([side[None], value[:-1]], axis=0)
                else:
                    value = jnp.concatenate([value[1:], side[None]], axis=0)
            pops_out[q] = value
            fresh.append(value)
        density, momentum = moments(fresh)
        inverse = 1.0 / density
        for a in range(3):
            out_flow[step, :, a] = (momentum[a] + 0.5 * force[a]) * inverse
        sends = flow_copies(step)
        for x in sends:
            x.start()
        for x in sends:
            x.wait_recv()
        R = {dv: recv_flow[d][step] for d, dv in enumerate(DIRS)}
        wide[0:rows_x, :, 0] = out_flow[step]
        wide[0:rows_x, :, 1] = jnp.where(low_rows, R[0, -1], R[0, 1])
        wide[rows_x : rows_x + 2, :, 0] = R[-1, 0]
        wide[rows_x : rows_x + 2, :, 1] = jnp.where(low_rows, R[-1, -1], R[-1, 1])
        wide[rows_x + 2 :, :, 0] = R[1, 0]
        wide[rows_x + 2 :, :, 1] = jnp.where(low_rows, R[1, -1], R[1, 1])
        wide_high, wide_low = split(wide[...].reshape(planes * 3 * 16, depth))
        twice = jnp.concatenate([wide_high, wide_high], axis=1)
        along = mm(twice, deep, NN) + mm(wide_low, deep_high, NN)
        along = along.reshape(planes, 3, 16, vertices)
        drift = []
        for a in range(3):
            acc = along[0, a] * table_x[0:1]
            for i, x in enumerate(order[1:], 1):
                acc = acc + along[i, a] * table_x[x : x + 1]
            drift.append(jnp.sum(acc * table_y, axis=0, keepdims=True))
        off[...] = now + live * jnp.concatenate(drift, axis=0)
        return carry

    lax.fori_loop(0, SUBSTEPS, substep, 0)

    for m in range(slots):
        offset_out[:, m, :] = off[:, m * padded : (m + 1) * padded]

    def drain(step, carry):
        for x in force_copies(step) + pops_copies(step) + flow_copies(step):
            x.wait_send()
        return carry

    lax.fori_loop(0, SUBSTEPS, drain, 0)


def local(mesh, populations, solid, base_cell, offset, rest, stiffness, occupied, triangles):
    rows_x, rows_y, depth = populations.shape[1:]
    slots, padded = offset.shape[3:]
    assert rows_y == 8 and 3 <= rows_x <= 5 and depth & (depth - 1) == 0
    vertices, planes, faces = slots * padded, rows_x + 3, triangles.shape[0]
    S = SUBSTEPS
    f32, bf16 = jnp.float32, jnp.bfloat16
    tile = (8, depth)
    n_force = {1: 2, -1: 1, 0: rows_x}
    n_flow = {1: 1, -1: 2, 0: rows_x}
    pop_shapes = [(5,)] * 2 + [(rows_x,)] * 2 + [()] * 4
    V = lambda shape, dtype=f32: pltpu.VMEM(shape, dtype)
    scratch = [
        V((padded, faces), bf16), V((2, padded, padded), bf16), V((3, vertices)),
        V((2, planes * 48, vertices), bf16), V((S, planes, 3, 2) + tile),
        V((8, depth)), V((S, rows_x, 3) + tile), V((planes, 3, 2) + tile),
    ]
    scratch += [V((S, n_force[sx], 3) + tile) for sx, sy in DIRS]
    scratch += [V((S,) + p + tile) for p in pop_shapes]
    scratch += [V((S, n_flow[sx], 3) + tile) for sx, sy in DIRS]
    scratch += [V((S,) + p + tile) for p in pop_shapes]
    scratch += [pltpu.SemaphoreType.DMA((S, 3, 8)), pltpu.SemaphoreType.DMA((S, 3, 8))]
    vmem = pl.BlockSpec(memory_space=pltpu.VMEM)
    smem = pl.BlockSpec(memory_space=pltpu.SMEM)
    small = (3, slots, padded)
    pops, moved = pl.pallas_call(
        functools.partial(body_kernel, mesh.shape["gx"], mesh.shape["gy"]),
        out_shape=(
            jax.ShapeDtypeStruct(populations.shape, f32),
            jax.ShapeDtypeStruct(small, f32),
        ),
        in_specs=[vmem] * 5 + [smem] * 2 + [vmem],
        out_specs=(vmem, vmem),
        scratch_shapes=scratch,
        compiler_params=pltpu.CompilerParams(
            collective_id=0, has_side_effects=True, vmem_limit_bytes=60 * 1024 * 1024
        ),
    )(
        populations, solid, base_cell.reshape(small), offset.reshape(small), rest.reshape(small),
        stiffness.reshape(slots), occupied.reshape(slots), triangles.T,
    )
    return pops, moved.reshape(offset.shape)


def solution(mesh):
    in_specs = (
        P(None, "gx", "gy", None),
        P("gx", "gy", None),
        P(None, "gx", "gy", None, None),
        P(None, "gx", "gy", None, None),
        P(None, "gx", "gy", None, None),
        P("gx", "gy", None),
        P("gx", "gy", None),
        P(),
    )
    out_specs = (P(None, "gx", "gy", None), P(None, "gx", "gy", None, None))
    return jax.shard_map(
        functools.partial(local, mesh), mesh=mesh, in_specs=in_specs, out_specs=out_specs,
        check_vma=False,
    )
```

profile of v0, /device:TPU:0, one launch (start us, length us, event | category | flops | bytes accessed | tf_op | source)
XLA Modules:
  0.0 64.7 jit_solution(3396484059433493507)
XLA Ops:
  0.6 61.8 %shard_map.95 = (f32[19,4,8,128]{3,2,1,0:T(8,128)}, f32[3,2,768]{2,1,0:T(2,128)}) custom-call(f32[19,4,8,128]{3,2,1,0:T(8,128)} %pops_ref.1, s32[4,8,128]{2,1,0:T(8,128)} %solid_ref.1, s32[3,2,768]{2,1,0:T(2,128)} %bitcast.10, f32[3,2,768]{2,1,0:T(2,128)} %bitcast.11, f32[3,2,768]{2,1,0:T(2,128)} %bitcast.12, f32[2]{0:T(128)} %bitcast.14, s32[2]{0:T(128)} %bitcast.15, ...), custom_call_target="tpu_custom_call" | custom-call | tf_op jit(solution)/shard_map/pallas_call | solution.py:329
  62.4 0.0 copy-start
  62.4 1.7 %copy.13 = f32[19,4,8,128]{3,2,1,0:T(8,128)} copy(f32[19,4,8,128]{3,2,1,0:T(8,128)} %get-tuple-element.10) | data formatting | bytes 622592
  64.1 0.0 copy-done
  64.1 0.6 copy.14
Async XLA Ops:
  62.4 1.7 %copy-start = (f32[3,2,768]{2,1,0:T(2,128)S(1)}, f32[3,2,768]{2,1,0:T(2,128)}, u32[]{:S(2)}) copy-start(f32[3,2,768]{2,1,0:T(2,128)} %get-tuple-element.5) | copy-start | bytes 55300
where the time goes:
time: 64.9 us; the launch traced here: 64.7 us
  Pallas kernels  61.8 us (95%)
  local copies, waits for them, and re-layouts  2.32 us (4%)
  between operations  0.65 us (1%)
    pallas_call x1, Pallas kernels, local(): pl.pallas_call(functools.partial(body_kernel, mesh.shape['gx'], mesh.shap...  61.8 us
    unnamed x4, local copies, waits for them, and re-layouts  2.32 us

commit v1 on v0

--- a/solution.py
+++ b/solution.py
@@ -99,16 +99,68 @@
     return x if shift == 0 else pltpu.roll(x, shift, axis)
 
 
+def row_mask(start, rows, depth):
+    sub = lax.broadcasted_iota(jnp.int32, (8, depth), 0)
+    return ((sub - start) & 7) < rows
+
+
+def pack(tiles, start, rows):
+    per, out = 8 // rows, []
+    for g in range(0, len(tiles), per):
+        acc = tiles[g]
+        for k, tile in enumerate(tiles[g + 1 : g + per], 1):
+            mask = row_mask(start + k * rows, rows, tile.shape[1])
+            acc = jnp.where(mask, roll(tile, k * rows, 0), acc)
+        out.append(acc)
+    return out
+
+
+def unpack(load, count, rows):
+    per = 8 // rows
+    return [roll(load(k // per), -(k % per) * rows, 0) for k in range(count)]
+
+
+def packed(count, rows):
+    return -(-count // (8 // rows))
+
+
+def force_planes(sx, rows_x):
+    return {1: [rows_x, rows_x + 1], -1: [-1], 0: list(range(rows_x))}[sx]
+
+
+def moment_planes(sx, rows_x):
+    return {1: [rows_x - 1, rows_x], -1: [-1, 0, 1], 0: list(range(-1, rows_x + 1))}[sx]
+
+
+def landing(x, sx, rows_x):
+    return x - sx * rows_x
+
+
+def force_size(sx, sy, rows_x):
+    n = 3 * len(force_planes(sx, rows_x))
+    return {0: n, 1: packed(n, 2), -1: packed(n, 1)}[sy]
+
+
+def moment_size(sx, sy, rows_x):
+    n = 4 * len(moment_planes(sx, rows_x))
+    return {0: n + packed(n, 2), 1: packed(n, 2), -1: packed(n, 1) + packed(n, 2)}[sy]
+
+
+def total_of(parts):
+    return functools.reduce(lambda a, b: a + b, parts)
+
+
 def body_kernel(
     peers_x, peers_y,
     pops_ref, solid_ref, base_ref, offset_ref, rest_ref, stiff_ref, occ_ref, tri_ref,
     pops_out, offset_out,
-    inc, lap, off, spread, grid, out_pops, out_flow, wide,
+    inc, lap, off, spread, moved_ref, wide,
     *scratch,
 ):
-    recv_force, recv_pops, recv_flow = scratch[0:8], scratch[8:16], scratch[16:24]
-    send_px, send_py, send_pc = scratch[24:26], scratch[26:28], scratch[28:32]
-    send_sem, recv_sem = scratch[32:34]
+    recv_force, recv_pops, recv_mom = scratch[0:8], scratch[8:16], scratch[16:24]
+    send_force, send_pops, send_mom = scratch[24:32], scratch[32:40], scratch[40:48]
+    send_px, send_py, send_pc = send_pops[0:2], send_pops[2:4], send_pops[4:8]
+    send_sem, recv_sem = scratch[48:50]
     rows_x = pops_ref.shape[1]
     depth = pops_ref.shape[3]
     slots, padded = base_ref.shape[1], base_ref.shape[2]
@@ -156,23 +208,38 @@
             recv_sem=recv_sem.at[step, stage, d], device_id=peer[d], device_id_type=MESH,
         )
 
-    def force_copies(step):
-        part = {1: pl.ds(rows_x, 2), -1: pl.ds(rows_x + 2, 1), 0: pl.ds(0, rows_x)}
-        return [
-            copy(step, 0, d, grid.at[step, part[sx], :, 0 if sy == 0 else 1], recv_force[d])
-            for d, (sx, sy) in enumerate(DIRS)
-        ]
-
-    def pops_copies(step):
-        src = list(send_px) + list(send_py) + list(send_pc)
-        return [copy(step, 1, d, src[d].at[step], recv_pops[d]) for d in range(8)]
-
-    def flow_copies(step):
-        part = {1: pl.ds(rows_x - 1, 1), -1: pl.ds(0, 2), 0: pl.ds(0, rows_x)}
-        return [
-            copy(step, 2, d, out_flow.at[step, part[sx]], recv_flow[d])
-            for d, (sx, sy) in enumerate(DIRS)
-        ]
+    groups = ((send_force, recv_force), (send_mom, recv_mom), (send_pops, recv_pops))
+
+    def copies(step, stage):
+        src, dst = groups[stage]
+        return [copy(step, stage, d, src[d].at[step], dst[d]) for d in (4, 5, 6, 7, 2, 3, 0, 1)]
+
+    def launch(step, stage):
+        for x in copies(step, stage):
+            x.start()
+
+    def arrive(step, stage):
+        for x in copies(step, stage):
+            x.wait_recv()
+
+    def finish_pops(step):
+        arrive(step, 2)
+        from_y = {1: recv_pops[2][step], -1: recv_pops[3][step]}
+        for q in range(19):
+            sx, sy, _ = VELOCITIES[q]
+            value = moved_ref[q]
+            edge_row = sub == (0 if sy == 1 else 7)
+            if sy:
+                value = jnp.where(edge_row, roll(from_y[sy], -YS[sy].index(q), 1), value)
+            if sx:
+                side = recv_pops[0 if sx == 1 else 1][step, XS[sx].index(q)]
+                if sy:
+                    side = jnp.where(edge_row, recv_pops[DIRS.index((sx, sy))][step], side)
+                if sx == 1:
+                    value = jnp.concatenate([side[None], value[:-1]], axis=0)
+                else:
+                    value = jnp.concatenate([value[1:], side[None]], axis=0)
+            pops_out[q] = value
 
     def substep(step, carry):
         now = off[...]
@@ -204,82 +271,154 @@
                 spread[1, row : row + 16, :] = low
         first = mm(spread[0], deep, NT)
         total = first[:, :depth] + first[:, depth:] + mm(spread[1], deep_high, NT)
-        grid[step] = total.reshape(planes, 3, 2, 8, depth)
-        sends = force_copies(step)
-        for x in sends:
-            x.start()
-        for x in sends:
-            x.wait_recv()
-        R = {dv: recv_force[d][step] for d, dv in enumerate(DIRS)}
-        low_rows = sub < 4
-        total = grid[step, 0:rows_x, :, 0] + jnp.where(low_rows, R[0, 1], R[0, -1])
-        left = R[1, 0] + jnp.where(low_rows, R[1, 1], R[1, -1])
-        right = R[-1, 0] + jnp.where(low_rows, R[-1, 1], R[-1, -1])
-        total = jnp.concatenate(
-            [total[0:2] + left, total[2 : rows_x - 1], total[rows_x - 1 :] + right], axis=0
-        )
-        force = [total[:, a] for a in range(3)]
+        place = {x % (rows_x + 3): i for i, x in enumerate(list(range(rows_x + 2)) + [-1])}
+
+        def tile_of(x, a, t):
+            row = (3 * place[x % (rows_x + 3)] + a) * 16 + 8 * t
+            return total[row : row + 8]
+
+        for d, (sx, sy) in enumerate(DIRS):
+            tiles = [
+                tile_of(x, a, 0 if sy == 0 else 1)
+                for x in force_planes(sx, rows_x) for a in range(3)
+            ]
+            if sy:
+                tiles = pack(tiles, 0 if sy == 1 else 7, 2 if sy == 1 else 1)
+            for k, tile in enumerate(tiles):
+                send_force[d][step, k] = tile
+        launch(step, 0)
+
+        @pl.when(step > 0)
+        def _():
+            finish_pops(step - 1)
+
+        arrive(step, 0)
+        parts = {(x, a): [tile_of(x, a, 0)] for x in range(rows_x) for a in range(3)}
+        for d, (sx, sy) in enumerate(DIRS):
+            names = [
+                (landing(x, sx, rows_x), a) for x in force_planes(sx, rows_x) for a in range(3)
+            ]
+            load = lambda k, d=d: recv_force[d][step, k]
+            if sy == 0:
+                tiles = [load(k) for k in range(len(names))]
+            else:
+                start, rows = (0, 2) if sy == 1 else (7, 1)
+                mask = row_mask(start, rows, depth)
+                tiles = [jnp.where(mask, t, 0.0) for t in unpack(load, len(names), rows)]
+            for name, tile in zip(names, tiles):
+                parts[name].append(tile)
+        force = [
+            jnp.stack([total_of(parts[x, a]) for x in range(rows_x)]) for a in range(3)
+        ]
 
         relaxed = collide([pops_out[q] for q in range(19)], force, solid_ref[...] != 0)
         moved = [
             roll(roll(relaxed[q], VELOCITIES[q][2], 2), VELOCITIES[q][1], 1) for q in range(19)
         ]
+        for q in range(19):
+            moved_ref[q] = moved[q]
+        nothing = jnp.zeros((1, 8, depth), jnp.float32)
+        rho, mz = {}, {}
+        for cx in (-1, 0, 1):
+            for cy in (-1, 0, 1):
+                members = [q for q in range(19) if VELOCITIES[q][:2] == (cx, cy)]
+                pad = lambda v: jnp.concatenate(
+                    [nothing] * (1 + cx) + [v] + [nothing] * (1 - cx), axis=0
+                )
+                rho[cx, cy] = pad(total_of([moved[q] for q in members]))
+                up = [moved[q] for q in members if VELOCITIES[q][2] == 1]
+                down = [moved[q] for q in members if VELOCITIES[q][2] == -1]
+                if up:
+                    mz[cx, cy] = pad(total_of(up) - total_of(down))
+        first_row, last_row = sub == 0, sub == 7
+        own = {}
+        zero = jnp.zeros((rows_x + 2, 8, depth), jnp.float32)
+        fields = []
+        for cy in (0, 1, -1):
+            dens = rho[-1, cy] + rho[0, cy] + rho[1, cy]
+            deep_m = [mz[cx, cy] for cx in (-1, 0, 1) if (cx, cy) in mz]
+            fields.append((
+                dens, rho[1, cy] - rho[-1, cy], zero if cy == 0 else cy * dens, total_of(deep_m)
+            ))
+        for c in range(4):
+            mid, up, down = (fields[g][c] for g in range(3))
+            near = mid + jnp.where(first_row, 0.0, up) + jnp.where(last_row, 0.0, down)
+            if c:
+                half = 0.5 * force[c - 1]
+                near = near + jnp.concatenate([nothing, half, nothing], axis=0)
+            far = jnp.where(first_row, up, jnp.where(last_row, down, 0.0))
+            for x in range(-1, rows_x + 1):
+                own[x, c] = (near[x + 1], far[x + 1])
+        for d, (sx, sy) in enumerate(DIRS):
+            names = [(x, c) for x in moment_planes(sx, rows_x) for c in range(4)]
+            near, far = [own[n][0] for n in names], [own[n][1] for n in names]
+            if sy == 0:
+                tiles = near + pack(far, 7, 2)
+            elif sy == 1:
+                tiles = pack([jnp.where(last_row, a, b) for a, b in zip(near, far)], 7, 2)
+            else:
+                tiles = pack(far, 7, 1) + pack(near, 0, 2)
+            for k, tile in enumerate(tiles):
+                send_mom[d][step, k] = tile
+        launch(step, 1)
         for n, sx in enumerate((1, -1)):
             edge = rows_x - 1 if sx == 1 else 0
             for k, q in enumerate(XS[sx]):
                 send_px[n][step, k] = moved[q][edge]
         for n, sy in enumerate((1, -1)):
-            packed = moved[YS[sy][0]]
+            rows_kept = moved[YS[sy][0]]
             start = 0 if sy == 1 else 7
             for k, q in enumerate(YS[sy][1:], 1):
-                packed = jnp.where(sub == (start + k) % 8, roll(moved[q], k, 1), packed)
-            send_py[n][step] = packed
+                rows_kept = jnp.where(sub == (start + k) % 8, roll(moved[q], k, 1), rows_kept)
+            send_py[n][step] = rows_kept
         for n, (sx, sy) in enumerate(DIRS[4:]):
             send_pc[n][step] = moved[CORNER[sx, sy]][rows_x - 1 if sx == 1 else 0]
-        sends = pops_copies(step)
-        for x in sends:
-            x.start()
-        for x in sends:
-            x.wait_recv()
-        from_y = {1: recv_pops[2][step], -1: recv_pops[3][step]}
-        fresh = []
-        for q in range(19):
-            sx, sy, _ = VELOCITIES[q]
-            value = moved[q]
-            edge_row = sub == (0 if sy == 1 else 7)
-            if sy:
-                value = jnp.where(edge_row, roll(from_y[sy], -YS[sy].index(q), 1), value)
-            if sx:
-                side = recv_pops[0 if sx == 1 else 1][step, XS[sx].index(q)]
-                if sy:
-                    side = jnp.where(edge_row, recv_pops[DIRS.index((sx, sy))][step], side)
-                if sx == 1:
-                    value = jnp.concatenate([side[None], value[:-1]], axis=0)
-                else:
-                    value = jnp.concatenate([value[1:], side[None]], axis=0)
-            pops_out[q] = value
-            fresh.append(value)
-        density, momentum = moments(fresh)
-        inverse = 1.0 / density
-        for a in range(3):
-            out_flow[step, :, a] = (momentum[a] + 0.5 * force[a]) * inverse
-        sends = flow_copies(step)
-        for x in sends:
-            x.start()
-        for x in sends:
-            x.wait_recv()
-        R = {dv: recv_flow[d][step] for d, dv in enumerate(DIRS)}
-        wide[0:rows_x, :, 0] = out_flow[step]
-        wide[0:rows_x, :, 1] = jnp.where(low_rows, R[0, -1], R[0, 1])
-        wide[rows_x : rows_x + 2, :, 0] = R[-1, 0]
-        wide[rows_x : rows_x + 2, :, 1] = jnp.where(low_rows, R[-1, -1], R[-1, 1])
-        wide[rows_x + 2 :, :, 0] = R[1, 0]
-        wide[rows_x + 2 :, :, 1] = jnp.where(low_rows, R[1, -1], R[1, 1])
+        launch(step, 2)
+        arrive(step, 1)
+        reach = [x for x in range(rows_x + 2)] + [-1]
+        near = {(x, c): [] for x in reach for c in range(4)}
+        far = {(x, c): [] for x in reach for c in range(4)}
+        for name, (a, b) in own.items():
+            near[name].append(a)
+            far[name].append(b)
+        two, edges, one = row_mask(0, 2, depth), row_mask(7, 2, depth), row_mask(7, 1, depth)
+        for d, (sx, sy) in enumerate(DIRS):
+            names = [
+                (landing(x, sx, rows_x), c)
+                for x in moment_planes(sx, rows_x) for c in range(4)
+            ]
+            count = len(names)
+            load = lambda k, d=d: recv_mom[d][step, k]
+            if sy == 0:
+                a = [load(k) for k in range(count)]
+                b = unpack(lambda k: load(count + k), count, 2)
+                b = [jnp.where(edges, t, 0.0) for t in b]
+            elif sy == 1:
+                both_rows = unpack(load, count, 2)
+                a = [jnp.where(first_row, t, 0.0) for t in both_rows]
+                b = [jnp.where(last_row, t, 0.0) for t in both_rows]
+            else:
+                skip = packed(count, 1)
+                a = [jnp.where(one, t, 0.0) for t in unpack(load, count, 1)]
+                b = unpack(lambda k: load(skip + k), count, 2)
+                b = [jnp.where(two, t, 0.0) for t in b]
+            for name, p, r in zip(names, a, b):
+                near[name].append(p)
+                far[name].append(r)
+        used = row_mask(7, 3, depth)
+        for i, x in enumerate(reach):
+            for t, side in enumerate((near, far)):
+                dens = total_of(side[x, 0])
+                if t:
+                    dens = jnp.where(used, dens, 1.0)
+                inverse = 1.0 / dens
+                for a in range(3):
+                    wide[i, a, t] = total_of(side[x, a + 1]) * inverse
         wide_high, wide_low = split(wide[...].reshape(planes * 3 * 16, depth))
         twice = jnp.concatenate([wide_high, wide_high], axis=1)
         along = mm(twice, deep, NN) + mm(wide_low, deep_high, NN)
         along = along.reshape(planes, 3, 16, vertices)
-        drift = []
+        drift, order = [], list(range(rows_x + 2)) + [7]
         for a in range(3):
             acc = along[0, a] * table_x[0:1]
             for i, x in enumerate(order[1:], 1):
@@ -289,13 +428,15 @@
         return carry
 
     lax.fori_loop(0, SUBSTEPS, substep, 0)
+    finish_pops(SUBSTEPS - 1)
 
     for m in range(slots):
         offset_out[:, m, :] = off[:, m * padded : (m + 1) * padded]
 
     def drain(step, carry):
-        for x in force_copies(step) + pops_copies(step) + flow_copies(step):
-            x.wait_send()
+        for stage in range(3):
+            for x in copies(step, stage):
+                x.wait_send()
         return carry
 
     lax.fori_loop(0, SUBSTEPS, drain, 0)
@@ -309,19 +450,17 @@
     S = SUBSTEPS
     f32, bf16 = jnp.float32, jnp.bfloat16
     tile = (8, depth)
-    n_force = {1: 2, -1: 1, 0: rows_x}
-    n_flow = {1: 1, -1: 2, 0: rows_x}
     pop_shapes = [(5,)] * 2 + [(rows_x,)] * 2 + [()] * 4
     V = lambda shape, dtype=f32: pltpu.VMEM(shape, dtype)
     scratch = [
         V((padded, faces), bf16), V((2, padded, padded), bf16), V((3, vertices)),
-        V((2, planes * 48, vertices), bf16), V((S, planes, 3, 2) + tile),
-        V((8, depth)), V((S, rows_x, 3) + tile), V((planes, 3, 2) + tile),
+        V((2, planes * 48, vertices), bf16),
+        V((19, rows_x) + tile), V((planes, 3, 2) + tile),
     ]
-    scratch += [V((S, n_force[sx], 3) + tile) for sx, sy in DIRS]
-    scratch += [V((S,) + p + tile) for p in pop_shapes]
-    scratch += [V((S, n_flow[sx], 3) + tile) for sx, sy in DIRS]
-    scratch += [V((S,) + p + tile) for p in pop_shapes]
+    for _ in ("receive", "send"):
+        scratch += [V((S, force_size(*d, rows_x)) + tile) for d in DIRS]
+        scratch += [V((S,) + p + tile) for p in pop_shapes]
+        scratch += [V((S, moment_size(*d, rows_x)) + tile) for d in DIRS]
     scratch += [pltpu.SemaphoreType.DMA((S, 3, 8)), pltpu.SemaphoreType.DMA((S, 3, 8))]
     vmem = pl.BlockSpec(memory_space=pltpu.VMEM)
     smem = pl.BlockSpec(memory_space=pltpu.SMEM)

time: 64.9 us -> 46.2 us (0.71)
  Pallas kernels: 61.8 us -> 43.1 us
    pallas_call x1, Pallas kernels: 61.8 us -> 43.1 us  [local(): pl.pallas_call(functools.partial(body_kernel, mesh.shape['gx'], mesh.shap...]
where the time goes in v1:
time: 46.2 us; the launch traced here: 46.1 us
  Pallas kernels  43.1 us (93%)
  local copies, waits for them, and re-layouts  2.32 us (5%)
  between operations  0.65 us (1%)
    pallas_call x1, Pallas kernels, local(): pl.pallas_call(functools.partial(body_kernel, mesh.shape['gx'], mesh.shap...  43.1 us
    unnamed x4, local copies, waits for them, and re-layouts  2.32 us

profile of v1, /device:TPU:0, one launch (start us, length us, event | category | flops | bytes accessed | tf_op | source)
XLA Modules:
  0.0 46.1 jit_solution(11316047917678477061)
XLA Ops:
  0.6 43.1 %shard_map.95 = (f32[19,4,8,128]{3,2,1,0:T(8,128)}, f32[3,2,768]{2,1,0:T(2,128)}) custom-call(f32[19,4,8,128]{3,2,1,0:T(8,128)} %pops_ref.1, s32[4,8,128]{2,1,0:T(8,128)} %solid_ref.1, s32[3,2,768]{2,1,0:T(2,128)} %bitcast.10, f32[3,2,768]{2,1,0:T(2,128)} %bitcast.11, f32[3,2,768]{2,1,0:T(2,128)} %bitcast.12, f32[2]{0:T(128)} %bitcast.14, s32[2]{0:T(128)} %bitcast.15, ...), custom_call_target="tpu_custom_call" | custom-call | tf_op jit(solution)/shard_map/pallas_call | solution.py:468
  43.8 0.0 copy-start
  43.8 1.7 %copy.13 = f32[19,4,8,128]{3,2,1,0:T(8,128)} copy(f32[19,4,8,128]{3,2,1,0:T(8,128)} %get-tuple-element.10) | data formatting | bytes 622592
  45.5 0.0 copy-done
  45.5 0.6 %copy.14 = f32[3,1,1,2,768]{4,3,2,1,0:T(2,128)} copy(f32[3,1,1,2,768]{4,3,2,1,0:T(2,128)S(1)} %bitcast.13) | data formatting | bytes 36864
Async XLA Ops:
  43.8 1.7 %copy-start = (f32[3,2,768]{2,1,0:T(2,128)S(1)}, f32[3,2,768]{2,1,0:T(2,128)}, u32[]{:S(2)}) copy-start(f32[3,2,768]{2,1,0:T(2,128)} %get-tuple-element.5) | copy-start | bytes 55300

commit v2 on v1

--- a/solution.py
+++ b/solution.py
@@ -160,7 +160,7 @@
     recv_force, recv_pops, recv_mom = scratch[0:8], scratch[8:16], scratch[16:24]
     send_force, send_pops, send_mom = scratch[24:32], scratch[32:40], scratch[40:48]
     send_px, send_py, send_pc = send_pops[0:2], send_pops[2:4], send_pops[4:8]
-    send_sem, recv_sem = scratch[48:50]
+    send_sem, recv_sem, load_sem = scratch[48:51]
     rows_x = pops_ref.shape[1]
     depth = pops_ref.shape[3]
     slots, padded = base_ref.shape[1], base_ref.shape[2]
@@ -169,6 +169,8 @@
     ix, iy = lax.axis_index("gx"), lax.axis_index("gy")
     peer = [((ix + sx + peers_x) % peers_x, (iy + sy + peers_y) % peers_y) for sx, sy in DIRS]
 
+    load_pops = pltpu.make_async_copy(pops_ref, pops_out, load_sem)
+    load_pops.start()
     barrier = pltpu.get_barrier_semaphore()
     for p in peer:
         pl.semaphore_signal(barrier, inc=1, device_id=p, device_id_type=MESH)
@@ -198,8 +200,8 @@
         [jnp.full((1, padded), stiff_ref[m]) for m in range(slots)], axis=1
     )
     off[...] = flat(offset_ref)
-    pops_out[...] = pops_ref[...]
     sub = lax.broadcasted_iota(jnp.int32, (8, depth), 0)
+    load_pops.wait()
     pl.semaphore_wait(barrier, len(peer))
 
     def copy(step, stage, d, src, dst):
@@ -212,11 +214,20 @@
 
     def copies(step, stage):
         src, dst = groups[stage]
-        return [copy(step, stage, d, src[d].at[step], dst[d]) for d in (4, 5, 6, 7, 2, 3, 0, 1)]
+        return [copy(step, stage, d, src[d].at[step], dst[d]) for d in range(8)]
 
     def launch(step, stage):
-        for x in copies(step, stage):
-            x.start()
+        sends = copies(step, stage)
+
+        @pl.when(iy % 2 == 1)
+        def _():
+            for d in (4, 6, 2, 5, 7, 3, 0, 1):
+                sends[d].start()
+
+        @pl.when(iy % 2 == 0)
+        def _():
+            for d in (5, 7, 3, 4, 6, 2, 0, 1):
+                sends[d].start()
 
     def arrive(step, stage):
         for x in copies(step, stage):
@@ -261,25 +272,32 @@
         table_y = table(16, base_y, [k[1:2] for k in kernels])
         deep_high, deep_low = split(table(depth, base_z, [k[2:3] for k in kernels]))
         deep = jnp.concatenate([deep_high, deep_low], axis=0)
-        order = list(range(rows_x + 2)) + [7]
-        for i, x in enumerate(order):
-            for a in range(3):
-                block = (force_v[a : a + 1] * table_x[x : x + 1]) * table_y
-                high, low = split(block)
-                row = (3 * i + a) * 16
+        tiles_of = {}
+
+        def spread_tiles(names, start):
+            for n in range(0, len(names), 2):
+                blocks = [
+                    (force_v[a : a + 1] * table_x[x & 7 : (x & 7) + 1])
+                    * table_y[8 * t : 8 * t + 8]
+                    for x, a, t in names[n : n + 2]
+                ]
+                high, low = split(jnp.concatenate(blocks, axis=0))
+                row = start + 8 * n
                 spread[0, row : row + 16, :] = high
                 spread[1, row : row + 16, :] = low
-        first = mm(spread[0], deep, NT)
-        total = first[:, :depth] + first[:, depth:] + mm(spread[1], deep_high, NT)
-        place = {x % (rows_x + 3): i for i, x in enumerate(list(range(rows_x + 2)) + [-1])}
-
-        def tile_of(x, a, t):
-            row = (3 * place[x % (rows_x + 3)] + a) * 16 + 8 * t
-            return total[row : row + 8]
-
+            stop = start + 8 * len(names)
+            first = mm(spread[0, start:stop], deep, NT)
+            total = first[:, :depth] + first[:, depth:]
+            total = total + mm(spread[1, start:stop], deep_high, NT)
+            for n, name in enumerate(names):
+                tiles_of[name] = total[8 * n : 8 * n + 8]
+
+        outer = [(x, a, t) for x in (rows_x, rows_x + 1, -1) for a in range(3) for t in (0, 1)]
+        outer += [(x, a, 1) for x in range(rows_x) for a in range(3)]
+        spread_tiles(outer, 0)
         for d, (sx, sy) in enumerate(DIRS):
             tiles = [
-                tile_of(x, a, 0 if sy == 0 else 1)
+                tiles_of[x, a, 0 if sy == 0 else 1]
                 for x in force_planes(sx, rows_x) for a in range(3)
             ]
             if sy:
@@ -287,13 +305,14 @@
             for k, tile in enumerate(tiles):
                 send_force[d][step, k] = tile
         launch(step, 0)
+        spread_tiles([(x, a, 0) for x in range(rows_x) for a in range(3)], 8 * len(outer))
 
         @pl.when(step > 0)
         def _():
             finish_pops(step - 1)
 
         arrive(step, 0)
-        parts = {(x, a): [tile_of(x, a, 0)] for x in range(rows_x) for a in range(3)}
+        parts = {(x, a): [tiles_of[x, a, 0]] for x in range(rows_x) for a in range(3)}
         for d, (sx, sy) in enumerate(DIRS):
             names = [
                 (landing(x, sx, rows_x), a) for x in force_planes(sx, rows_x) for a in range(3)
@@ -445,7 +464,7 @@
 def local(mesh, populations, solid, base_cell, offset, rest, stiffness, occupied, triangles):
     rows_x, rows_y, depth = populations.shape[1:]
     slots, padded = offset.shape[3:]
-    assert rows_y == 8 and 3 <= rows_x <= 5 and depth & (depth - 1) == 0
+    assert rows_y == 8 and rows_x == 4 and depth & (depth - 1) == 0
     vertices, planes, faces = slots * padded, rows_x + 3, triangles.shape[0]
     S = SUBSTEPS
     f32, bf16 = jnp.float32, jnp.bfloat16
@@ -462,6 +481,7 @@
         scratch += [V((S,) + p + tile) for p in pop_shapes]
         scratch += [V((S, moment_size(*d, rows_x)) + tile) for d in DIRS]
     scratch += [pltpu.SemaphoreType.DMA((S, 3, 8)), pltpu.SemaphoreType.DMA((S, 3, 8))]
+    scratch += [pltpu.SemaphoreType.DMA(())]
     vmem = pl.BlockSpec(memory_space=pltpu.VMEM)
     smem = pl.BlockSpec(memory_space=pltpu.SMEM)
     small = (3, slots, padded)
@@ -471,7 +491,7 @@
             jax.ShapeDtypeStruct(populations.shape, f32),
             jax.ShapeDtypeStruct(small, f32),
         ),
-        in_specs=[vmem] * 5 + [smem] * 2 + [vmem],
+        in_specs=[pl.BlockSpec(memory_space=pl.ANY)] + [vmem] * 4 + [smem] * 2 + [vmem],
         out_specs=(vmem, vmem),
         scratch_shapes=scratch,
         compiler_params=pltpu.CompilerParams(

time: 46.2 us -> 46.1 us (level)
  no operation moved by 1% of the time
where the time goes in v2:
time: 46.1 us; the launch traced here: 45.9 us
  Pallas kernels  43 us (93%)
  local copies, waits for them, and re-layouts  2.32 us (5%)
  between operations  0.65 us (1%)
    pallas_call x1, Pallas kernels, local(): pl.pallas_call(functools.partial(body_kernel, mesh.shape['gx'], mesh.shap...  43 us
    unnamed x4, local copies, waits for them, and re-layouts  2.32 us

profile of v2, /device:TPU:0, one launch (start us, length us, event | category | flops | bytes accessed | tf_op | source)
XLA Modules:
  0.0 45.9 jit_solution(15920366141719094032)
XLA Ops:
  0.6 43.0 %shard_map.95 = (f32[19,4,8,128]{3,2,1,0:T(8,128)}, f32[3,2,768]{2,1,0:T(2,128)}) custom-call(f32[19,4,8,128]{3,2,1,0:T(8,128)} %pops_ref.1, s32[4,8,128]{2,1,0:T(8,128)} %solid_ref.1, s32[3,2,768]{2,1,0:T(2,128)} %bitcast.10, f32[3,2,768]{2,1,0:T(2,128)} %bitcast.11, f32[3,2,768]{2,1,0:T(2,128)} %bitcast.12, f32[2]{0:T(128)} %bitcast.14, s32[2]{0:T(128)} %bitcast.15, ...), custom_call_target="tpu_custom_call" | custom-call | tf_op jit(solution)/shard_map/pallas_call | solution.py:488
  43.6 0.0 copy-start
  43.6 1.7 %copy.13 = f32[19,4,8,128]{3,2,1,0:T(8,128)} copy(f32[19,4,8,128]{3,2,1,0:T(8,128)} %get-tuple-element.10) | data formatting | bytes 622592
  45.3 0.0 copy-done
  45.3 0.6 %copy.14 = f32[3,1,1,2,768]{4,3,2,1,0:T(2,128)} copy(f32[3,1,1,2,768]{4,3,2,1,0:T(2,128)S(1)} %bitcast.13) | data formatting | bytes 36864
Async XLA Ops:
  43.6 1.7 %copy-start = (f32[3,2,768]{2,1,0:T(2,128)S(1)}, f32[3,2,768]{2,1,0:T(2,128)}, u32[]{:S(2)}) copy-start(f32[3,2,768]{2,1,0:T(2,128)} %get-tuple-element.5) | copy-start | bytes 55300

commit v3 on v2

--- a/solution.py
+++ b/solution.py
@@ -154,7 +154,7 @@
     peers_x, peers_y,
     pops_ref, solid_ref, base_ref, offset_ref, rest_ref, stiff_ref, occ_ref, tri_ref,
     pops_out, offset_out,
-    inc, lap, off, spread, moved_ref, wide,
+    lap, off, spread, moved_ref, wide,
     *scratch,
 ):
     recv_force, recv_pops, recv_mom = scratch[0:8], scratch[8:16], scratch[16:24]
@@ -175,10 +175,16 @@
     for p in peer:
         pl.semaphore_signal(barrier, inc=1, device_id=p, device_id_type=MESH)
 
-    ids = lax.broadcasted_iota(jnp.int32, inc.shape, 0)
-    hit = (ids == tri_ref[0:1, :]) | (ids == tri_ref[1:2, :]) | (ids == tri_ref[2:3, :])
-    inc[...] = jnp.where(hit, 1.0, 0.0).astype(jnp.bfloat16)
-    pairs = mm(inc[...], inc[...], NT)
+    faces = tri_ref.shape[1]
+    pairs = None
+    for start in range(0, faces, 256):
+        stop = min(start + 256, faces)
+        ids = lax.broadcasted_iota(jnp.int32, (base_ref.shape[2], stop - start), 0)
+        corner = [tri_ref[k : k + 1, start:stop] for k in range(3)]
+        hit = (ids == corner[0]) | (ids == corner[1]) | (ids == corner[2])
+        part = jnp.where(hit, 1.0, 0.0).astype(jnp.bfloat16)
+        part = mm(part, part, NT)
+        pairs = part if pairs is None else pairs + part
     same = lax.broadcasted_iota(jnp.int32, pairs.shape, 0) == lax.broadcasted_iota(
         jnp.int32, pairs.shape, 1
     )
@@ -202,7 +208,6 @@
     off[...] = flat(offset_ref)
     sub = lax.broadcasted_iota(jnp.int32, (8, depth), 0)
     load_pops.wait()
-    pl.semaphore_wait(barrier, len(peer))
 
     def copy(step, stage, d, src, dst):
         return pltpu.make_async_remote_copy(
@@ -304,6 +309,10 @@
                 tiles = pack(tiles, 0 if sy == 1 else 7, 2 if sy == 1 else 1)
             for k, tile in enumerate(tiles):
                 send_force[d][step, k] = tile
+        @pl.when(step == 0)
+        def _():
+            pl.semaphore_wait(barrier, len(peer))
+
         launch(step, 0)
         spread_tiles([(x, a, 0) for x in range(rows_x) for a in range(3)], 8 * len(outer))
 
@@ -465,14 +474,14 @@
     rows_x, rows_y, depth = populations.shape[1:]
     slots, padded = offset.shape[3:]
     assert rows_y == 8 and rows_x == 4 and depth & (depth - 1) == 0
-    vertices, planes, faces = slots * padded, rows_x + 3, triangles.shape[0]
+    vertices, planes = slots * padded, rows_x + 3
     S = SUBSTEPS
     f32, bf16 = jnp.float32, jnp.bfloat16
     tile = (8, depth)
     pop_shapes = [(5,)] * 2 + [(rows_x,)] * 2 + [()] * 4
     V = lambda shape, dtype=f32: pltpu.VMEM(shape, dtype)
     scratch = [
-        V((padded, faces), bf16), V((2, padded, padded), bf16), V((3, vertices)),
+        V((2, padded, padded), bf16), V((3, vertices)),
         V((2, planes * 48, vertices), bf16),
         V((19, rows_x) + tile), V((planes, 3, 2) + tile),
     ]

time: 46.1 us -> 45.4 us (0.985)
  Pallas kernels: 43 us -> 42.1 us
    pallas_call x1, Pallas kernels: 43 us -> 42.1 us  [local(): pl.pallas_call(functools.partial(body_kernel, mesh.shape['gx'], mesh.shap...]
where the time goes in v3:
time: 45.4 us; the launch traced here: 45.1 us
  Pallas kernels  42.1 us (93%)
  local copies, waits for them, and re-layouts  2.32 us (5%)
  between operations  0.65 us (1%)
    pallas_call x1, Pallas kernels, local(): pl.pallas_call(functools.partial(body_kernel, mesh.shape['gx'], mesh.shap...  42.1 us
    unnamed x4, local copies, waits for them, and re-layouts  2.32 us

profile of v3, /device:TPU:0, one launch (start us, length us, event | category | flops | bytes accessed | tf_op | source)
XLA Modules:
  0.0 45.1 jit_solution(5829549743429516956)
XLA Ops:
  0.6 42.1 %shard_map.95 = (f32[19,4,8,128]{3,2,1,0:T(8,128)}, f32[3,2,768]{2,1,0:T(2,128)}) custom-call(f32[19,4,8,128]{3,2,1,0:T(8,128)} %pops_ref.1, s32[4,8,128]{2,1,0:T(8,128)} %solid_ref.1, s32[3,2,768]{2,1,0:T(2,128)} %bitcast.10, f32[3,2,768]{2,1,0:T(2,128)} %bitcast.11, f32[3,2,768]{2,1,0:T(2,128)} %bitcast.12, f32[2]{0:T(128)} %bitcast.14, s32[2]{0:T(128)} %bitcast.15, ...), custom_call_target="tpu_custom_call" | custom-call | tf_op jit(solution)/shard_map/pallas_call | solution.py:497
  42.8 0.0 copy-start
  42.8 1.7 %copy.13 = f32[19,4,8,128]{3,2,1,0:T(8,128)} copy(f32[19,4,8,128]{3,2,1,0:T(8,128)} %get-tuple-element.10) | data formatting | bytes 622592
  44.5 0.0 copy-done
  44.5 0.6 %copy.14 = f32[3,1,1,2,768]{4,3,2,1,0:T(2,128)} copy(f32[3,1,1,2,768]{4,3,2,1,0:T(2,128)S(1)} %bitcast.13) | data formatting | bytes 36864
Async XLA Ops:
  42.8 1.7 %copy-start = (f32[3,2,768]{2,1,0:T(2,128)S(1)}, f32[3,2,768]{2,1,0:T(2,128)}, u32[]{:S(2)}) copy-start(f32[3,2,768]{2,1,0:T(2,128)} %get-tuple-element.5) | copy-start | bytes 55300

commit v4 on v3

--- a/solution.py
+++ b/solution.py
@@ -459,7 +459,7 @@
     finish_pops(SUBSTEPS - 1)
 
     for m in range(slots):
-        offset_out[:, m, :] = off[:, m * padded : (m + 1) * padded]
+        offset_out[:, m, :] = off[:, m * padded : (m + 1) * padded] - offset_ref[:, m, :]
 
     def drain(step, carry):
         for stage in range(3):
@@ -510,7 +510,7 @@
         populations, solid, base_cell.reshape(small), offset.reshape(small), rest.reshape(small),
         stiffness.reshape(slots), occupied.reshape(slots), triangles.T,
     )
-    return pops, moved.reshape(offset.shape)
+    return pops, offset + moved.reshape(offset.shape)
 
 
 def solution(mesh):

time: 45.4 us -> 46.2 us (1.018)
  other arithmetic: 0 us -> 1.34 us
  local copies, waits for them, and re-layouts: 2.32 us -> 1.71 us
    unnamed x0 -> x1, other arithmetic: none -> 1.34 us
    unnamed x4 -> x3, local copies, waits for them, and re-layouts: 2.32 us -> 1.71 us
where the time goes in v4:
time: 46.2 us; the launch traced here: 45.9 us
  Pallas kernels  42.2 us (91%)
  local copies, waits for them, and re-layouts  1.71 us (4%)
  other arithmetic  1.34 us (3%)
  between operations  0.66 us (1%)
    pallas_call x1, Pallas kernels, local(): pl.pallas_call(functools.partial(body_kernel, mesh.shape['gx'], mesh.shap...  42.2 us
    unnamed x3, local copies, waits for them, and re-layouts  1.71 us
    unnamed x1, other arithmetic  1.34 us

profile of v4, /device:TPU:0, one launch (start us, length us, event | category | flops | bytes accessed | tf_op | source)
XLA Modules:
  0.0 45.9 jit_solution(5348350507631627156)
XLA Ops:
  0.6 0.0 copy-start
  0.6 42.2 %shard_map.95 = (f32[19,4,8,128]{3,2,1,0:T(8,128)}, f32[3,2,768]{2,1,0:T(2,128)}) custom-call(f32[19,4,8,128]{3,2,1,0:T(8,128)} %pops_ref.1, s32[4,8,128]{2,1,0:T(8,128)} %solid_ref.1, s32[3,2,768]{2,1,0:T(2,128)} %bitcast.16, f32[3,2,768]{2,1,0:T(2,128)} %bitcast.14, f32[3,2,768]{2,1,0:T(2,128)} %bitcast.17, f32[2]{0:T(128)} %bitcast.18, s32[2]{0:T(128)} %bitcast.19, ...), custom_call_target="tpu_custom_call" | custom-call | tf_op jit(solution)/shard_map/pallas_call | solution.py:497
  42.8 0.0 copy-done
  42.8 1.3 %fusion = f32[3,1,1,2,768]{4,3,2,1,0:T(2,128)} fusion(f32[3,2,768]{2,1,0:T(2,128)} %get-tuple-element.5, f32[3,1,1,2,768]{4,3,2,1,0:T(2,128)S(1)} %copy-done), kind=kLoop, calls=%fused_computation.1 | loop fusion | flops 4608 | bytes 55296
  44.2 1.7 %copy.13 = f32[19,4,8,128]{3,2,1,0:T(8,128)} copy(f32[19,4,8,128]{3,2,1,0:T(8,128)} %get-tuple-element.10) | data formatting | bytes 622592
Async XLA Ops:
  0.6 42.2 %copy-start = (f32[3,1,1,2,768]{4,3,2,1,0:T(2,128)S(1)}, f32[3,1,1,2,768]{4,3,2,1,0:T(2,128)}, u32[]{:S(2)}) copy-start(f32[3,1,1,2,768]{4,3,2,1,0:T(2,128)} %param.11) | copy-start | bytes 55300
